TPU v7x, 32 devices: a whole 2x2x4 slice. The times are simulated.
32 devices in a mesh: dp: 8 (over z, y), head: 4 (over x, core).
Axes of the slice: x: 2, y: 2, z: 4, core: 2. Of those that a mesh axis runs over, the one named last changes fastest.
Arguments:
- tokens: bfloat16 [8, 6312, 768], P('dp', 'head'), may hold values from -6 to 6
- frames: int32 [8], P('dp'), may hold values from 4 to 16
- text_mask: int32 [8, 40], P('dp'), may hold values 0 or 1
- latents: bfloat16 [8, 128, 768], P('dp'), may hold values from -6 to 6
- cross_q: bfloat16 [768, 768], P('head'), may hold values from -0.21875 to 0.21875
- cross_kv: bfloat16 [2, 768, 768], P(None, 'head'), may hold values from -0.21875 to 0.21875
- cross_out: bfloat16 [768, 768], P('head'), may hold values from -3.5 to 3.5
- cross_up: bfloat16 [768, 3072], P(None, 'head'), may hold values from -0.21875 to 0.21875
- cross_down: bfloat16 [3072, 768], P('head'), may hold values from -0.109375 to 0.109375
- self_qkv: bfloat16 [3, 768, 768], P(None, 'head'), may hold values from -0.21875 to 0.21875
- self_out: bfloat16 [768, 768], P('head'), may hold values from -0.875 to 0.875
- self_up: bfloat16 [768, 3072], P(None, 'head'), may hold values from -0.21875 to 0.21875
- self_down: bfloat16 [3072, 768], P('head'), may hold values from -0.109375 to 0.109375
- head_bias: float32 [2, 2, 768], P(None, None, 'head'), may hold values from -1.8 to 1.8
- up_bias: float32 [2, 3072], P(None, 'head'), may hold values from -1.8 to 1.8
- out_bias: float32 [2, 2, 768], replicated, may hold values from -1.8 to 1.8
- norm_gain: float32 [5, 768], replicated, may hold values from 0.5 to 1.5
- norm_bias: float32 [5, 768], replicated, may hold values from -1.8 to 1.8
- latents_cot: float32 [8, 128, 768], P('dp'), may hold values from -6 to 6
Outputs:
- latents_out: float32 [8, 128, 768], P('dp')
- grad_tokens: bfloat16 [8, 6312, 768], P('dp', 'head')
- grad_latents: float32 [8, 128, 768], P('dp')
- grad_cross_q: float32 [768, 768], P('head', 'dp')
- grad_cross_kv: float32 [2, 768, 768], P(None, 'head', 'dp')
- grad_cross_out: float32 [768, 768], P('head', 'dp')
- grad_cross_up: float32 [768, 3072], P('dp', 'head')
- grad_cross_down: float32 [3072, 768], P('head', 'dp')
- grad_self_qkv: float32 [3, 768, 768], P(None, 'head', 'dp')
- grad_self_out: float32 [768, 768], P('head', 'dp')
- grad_self_up: float32 [768, 3072], P('dp', 'head')
- grad_self_down: float32 [3072, 768], P('head', 'dp')
- grad_head_bias: float32 [2, 2, 768], P(None, None, 'head')
- grad_up_bias: float32 [2, 3072], P(None, 'head')
- grad_out_bias: float32 [2, 2, 768], P(None, None, 'head')
- grad_norm_gain: float32 [5, 768], P(None, 'head')
- grad_norm_bias: float32 [5, 768], P(None, 'head')
Inputs may be any that keep to these rules, and one draw needn't show every extreme that they name: The patches of frames at or after frames[c] are padding.
All inputs are finite; a program needn't handle non-finite values. No bound on the sum of `text_mask` on one device may be relied on, other than what follows from the above.
Results may differ from a plain program's by a relative error of at most 0.018.
Values may be sent and summed in bfloat16 or wider, within the bound.
A program may use at most 128 MiB of HBM per device.

v0:
```python
from functools import partial
import jax
import jax.numpy as jnp
from jax import lax
from jax.sharding import PartitionSpec as P

HD = 64
P_SIZE = 392
F_MAX = 16
EPSILON = 1e-05
NEGATIVE = -1e30


def normed(tensor, gain_row, shift_row):
    row_mean = jnp.mean(tensor, axis=-1, keepdims=True)
    centered = tensor - row_mean
    spread = jnp.mean(centered * centered, axis=-1, keepdims=True)
    return centered * lax.rsqrt(spread + EPSILON) * gain_row + shift_row


def share_of(tensor, head_index, head_width):
    return lax.dynamic_slice_in_dim(tensor, head_index * head_width, head_width, tensor.ndim - 1)


def split_heads(tensor, heads_here):
    return tensor.reshape(
        tensor.shape[0], tensor.shape[1], heads_here, tensor.shape[2] // heads_here
    )


def merge_heads(tensor):
    return tensor.reshape(tensor.shape[0], tensor.shape[1], tensor.shape[2] * tensor.shape[3])


def join_heads(partial_sum):
    return lax.psum(partial_sum.astype(jnp.bfloat16), "head").astype(jnp.float32)


def join_back(partial_sum):
    return lax.psum(partial_sum.astype(jnp.bfloat16), "head").astype(jnp.float32)


def scores_of(queries, key_rows, usable):
    scores = jnp.einsum("qhe,khe->hqk", queries, key_rows, preferred_element_type=jnp.float32)
    return jnp.where(usable[None, None, :], scores, NEGATIVE)


def attend_parts(parts):
    queries, key_rows, values, usable = parts
    scores = scores_of(queries, key_rows, usable)
    row_max = jnp.max(scores, axis=-1, keepdims=True)
    powers = jnp.exp(scores - row_max)
    totals = jnp.sum(powers, axis=-1, keepdims=True)
    chances = (powers / totals).astype(jnp.bfloat16)
    mixture = jnp.einsum("hqk,khe->qhe", chances, values, preferred_element_type=jnp.float32)
    return (mixture.astype(jnp.bfloat16), row_max, totals)


def back_parts(parts):
    queries, key_rows, values, usable, row_max, totals, grad_mix = parts
    scores = scores_of(queries, key_rows, usable)
    chances = jnp.exp(scores - row_max) / totals
    rounded = chances.astype(jnp.bfloat16)
    grad_values = jnp.einsum(
        "hqk,qhe->khe", rounded, grad_mix, preferred_element_type=jnp.float32
    ).astype(jnp.bfloat16)
    grad_chances = jnp.einsum("qhe,khe->hqk", grad_mix, values, preferred_element_type=jnp.float32)
    inner_sum = jnp.sum(chances * grad_chances, axis=-1, keepdims=True)
    grad_scores = (chances * (grad_chances - inner_sum)).astype(jnp.bfloat16)
    grad_queries = jnp.einsum(
        "hqk,khe->qhe", grad_scores, key_rows, preferred_element_type=jnp.float32
    ).astype(jnp.bfloat16)
    grad_keys = jnp.einsum(
        "hqk,qhe->khe", grad_scores, queries, preferred_element_type=jnp.float32
    ).astype(jnp.bfloat16)
    return (grad_queries, grad_keys, grad_values)


def feed_forward(tensor, gain_row, shift_row, weight_up, bias_up, weight_down):
    hidden = normed(tensor, gain_row, shift_row).astype(jnp.bfloat16)
    pre_act = (
        jnp.einsum("cnd,df->cnf", hidden, weight_up, preferred_element_type=jnp.float32) + bias_up
    )
    activation = jax.nn.gelu(pre_act, approximate=True).astype(jnp.bfloat16)
    partial_sum = jnp.einsum(
        "cnf,fd->cnd", activation, weight_down, preferred_element_type=jnp.float32
    )
    return (join_heads(partial_sum), (hidden, pre_act, activation))


def feed_back(tensor, gain_row, shift_row, weight_up, weight_down, saved_acts, grad_out):
    hidden, pre_act, activation = saved_acts
    grad_branch = grad_out.astype(jnp.bfloat16)
    grad_weight_down = jnp.einsum(
        "cnf,cnd->fd", activation, grad_branch, preferred_element_type=jnp.float32
    )
    grad_act = jnp.einsum(
        "cnd,fd->cnf", grad_branch, weight_down, preferred_element_type=jnp.float32
    )
    unused, gelu_pull = jax.vjp(partial(jax.nn.gelu, approximate=True), pre_act)
    grad_pre = gelu_pull(grad_act)[0].astype(jnp.bfloat16)
    grad_weight_up = jnp.einsum("cnd,cnf->df", hidden, grad_pre, preferred_element_type=jnp.float32)
    grad_bias_up = jnp.sum(grad_pre.astype(jnp.float32), axis=(0, 1))
    grad_hidden = join_back(
        jnp.einsum("cnf,df->cnd", grad_pre, weight_up, preferred_element_type=jnp.float32)
    )
    unused_too, norm_pull = jax.vjp(normed, tensor, gain_row, shift_row)
    grad_tensor, grad_gain, grad_shift = norm_pull(grad_hidden)
    return (grad_tensor, grad_weight_up, grad_bias_up, grad_weight_down, grad_gain, grad_shift)


def local(
    tokens,
    frames,
    text_mask,
    latents,
    cross_q,
    cross_kv,
    cross_out,
    cross_up,
    cross_down,
    self_qkv,
    self_out,
    self_up,
    self_down,
    head_bias,
    up_bias,
    out_bias,
    norm_gain,
    norm_bias,
    latents_cot,
):
    head_index = lax.axis_index("head")
    head_width = cross_q.shape[0]
    heads_here = head_width // HD
    scaling = HD ** (-0.5)
    clips_here = tokens.shape[0]
    rows_here = tokens.shape[1]
    length = rows_here * lax.axis_size("head")
    position = jnp.arange(length, dtype=jnp.int32)
    text_full = jnp.concatenate(
        [jnp.zeros((clips_here, F_MAX * P_SIZE), jnp.int32), text_mask], axis=1
    )
    usable = (position[None, :] < frames[:, None] * P_SIZE) | (text_full == 1)
    gathered, weights_whole = (
        lax.all_gather(tokens, "head", axis=1, tiled=True),
        lax.all_gather(cross_kv, "head", axis=1, tiled=True),
    )
    full_rows = gathered.astype(jnp.float32)
    row_mean = jnp.mean(full_rows, axis=-1, keepdims=True)
    centered = full_rows - row_mean
    inverse = lax.rsqrt(jnp.mean(centered * centered, axis=-1, keepdims=True) + EPSILON)
    inputs = (centered * inverse * norm_gain[0] + norm_bias[0]).astype(jnp.bfloat16)
    key_value = jnp.einsum("cld,kwd->clkw", inputs, cross_kv, preferred_element_type=jnp.float32)
    key_rows = key_value[:, :, 0].astype(jnp.bfloat16)
    cross_values = (key_value[:, :, 1] + head_bias[0, 1]).astype(jnp.bfloat16)
    start_state = latents.astype(jnp.float32)
    latent_norm = normed(start_state, norm_gain[1], norm_bias[1]).astype(jnp.bfloat16)
    cross_queries = (
        (
            jnp.einsum("cnd,wd->cnw", latent_norm, cross_q, preferred_element_type=jnp.float32)
            + head_bias[0, 0]
        )
        * scaling
    ).astype(jnp.bfloat16)
    cross_parts = (
        split_heads(cross_queries, heads_here),
        split_heads(key_rows, heads_here),
        split_heads(cross_values, heads_here),
        usable,
    )
    cross_mix, cross_max, cross_totals = lax.map(attend_parts, cross_parts)
    cross_flat = merge_heads(cross_mix)
    after_cross = (
        start_state
        + join_heads(
            jnp.einsum("cnw,wd->cnd", cross_flat, cross_out, preferred_element_type=jnp.float32)
        )
        + out_bias[0, 0]
    )
    cross_branch, cross_saved = feed_forward(
        after_cross, norm_gain[2], norm_bias[2], cross_up, up_bias[0], cross_down
    )
    after_mlp = after_cross + cross_branch + out_bias[0, 1]
    self_norm = normed(after_mlp, norm_gain[3], norm_bias[3]).astype(jnp.bfloat16)
    triple = jnp.einsum("cnd,kwd->cnkw", self_norm, self_qkv, preferred_element_type=jnp.float32)
    self_queries = ((triple[:, :, 0] + head_bias[1, 0]) * scaling).astype(jnp.bfloat16)
    self_keys = triple[:, :, 1].astype(jnp.bfloat16)
    self_values = (triple[:, :, 2] + head_bias[1, 1]).astype(jnp.bfloat16)
    everyone = jnp.ones((clips_here, self_keys.shape[1]), dtype=bool)
    self_parts = (
        split_heads(self_queries, heads_here),
        split_heads(self_keys, heads_here),
        split_heads(self_values, heads_here),
        everyone,
    )
    self_mix, self_max, self_totals = lax.map(attend_parts, self_parts)
    self_flat = merge_heads(self_mix)
    after_self = (
        after_mlp
        + join_heads(
            jnp.einsum("cnw,wd->cnd", self_flat, self_out, preferred_element_type=jnp.float32)
        )
        + out_bias[1, 0]
    )
    self_branch, self_saved = feed_forward(
        after_self, norm_gain[4], norm_bias[4], self_up, up_bias[1], self_down
    )
    latents_out = after_self + self_branch + out_bias[1, 1]
    bias_self_mlp = jnp.sum(latents_cot, axis=(0, 1))
    grad_ln_four, grad_self_up, upbias_self, grad_self_down, gain_four, shift_four = feed_back(
        after_self, norm_gain[4], norm_bias[4], self_up, self_down, self_saved, latents_cot
    )
    grad_state = latents_cot + grad_ln_four
    bias_self_attn = jnp.sum(grad_state, axis=(0, 1))
    grad_attn_in = grad_state.astype(jnp.bfloat16)
    grad_self_out = jnp.einsum(
        "cnw,cnd->wd", self_flat, grad_attn_in, preferred_element_type=jnp.float32
    )
    grad_mix = jnp.einsum(
        "cnd,wd->cnw", grad_attn_in, self_out, preferred_element_type=jnp.float32
    ).astype(jnp.bfloat16)
    self_grads = lax.map(
        back_parts, self_parts + (self_max, self_totals, split_heads(grad_mix, heads_here))
    )
    grad_query_scaled = (merge_heads(self_grads[0]).astype(jnp.float32) * scaling).astype(
        jnp.bfloat16
    )
    grad_triple = jnp.stack(
        [grad_query_scaled, merge_heads(self_grads[1]), merge_heads(self_grads[2])], axis=2
    )
    grad_self_qkv = jnp.einsum(
        "cnd,cnkw->kwd", self_norm, grad_triple, preferred_element_type=jnp.float32
    )
    bias_self_q = jnp.sum(grad_triple[:, :, 0].astype(jnp.float32), axis=(0, 1))
    bias_self_v = jnp.sum(grad_triple[:, :, 2].astype(jnp.float32), axis=(0, 1))
    grad_self_in = join_back(
        jnp.einsum("cnkw,kwd->cnd", grad_triple, self_qkv, preferred_element_type=jnp.float32)
    )
    unused, norm_pull = jax.vjp(normed, after_mlp, norm_gain[3], norm_bias[3])
    grad_ln_three, gain_three, shift_three = norm_pull(grad_self_in)
    grad_state = grad_state + grad_ln_three
    bias_cross_mlp = jnp.sum(grad_state, axis=(0, 1))
    grad_ln_two, grad_cross_up, upbias_cross, grad_cross_down, gain_two, shift_two = feed_back(
        after_cross, norm_gain[2], norm_bias[2], cross_up, cross_down, cross_saved, grad_state
    )
    grad_state = grad_state + grad_ln_two
    bias_cross_attn = jnp.sum(grad_state, axis=(0, 1))
    grad_attn_in = grad_state.astype(jnp.bfloat16)
    grad_cross_out = jnp.einsum(
        "cnw,cnd->wd", cross_flat, grad_attn_in, preferred_element_type=jnp.float32
    )
    grad_mix = jnp.einsum(
        "cnd,wd->cnw", grad_attn_in, cross_out, preferred_element_type=jnp.float32
    ).astype(jnp.bfloat16)
    cross_grads = lax.map(
        back_parts, cross_parts + (cross_max, cross_totals, split_heads(grad_mix, heads_here))
    )
    grad_query_cross = (merge_heads(cross_grads[0]).astype(jnp.float32) * scaling).astype(
        jnp.bfloat16
    )
    grad_cross_q = jnp.einsum(
        "cnd,cnw->wd", latent_norm, grad_query_cross, preferred_element_type=jnp.float32
    )
    bias_cross_q = jnp.sum(grad_query_cross.astype(jnp.float32), axis=(0, 1))
    grad_latent_in = join_back(
        jnp.einsum("cnw,wd->cnd", grad_query_cross, cross_q, preferred_element_type=jnp.float32)
    )
    unused_too, latent_pull = jax.vjp(normed, start_state, norm_gain[1], norm_bias[1])
    grad_ln_one, gain_one, shift_one = latent_pull(grad_latent_in)
    grad_latents = grad_state + grad_ln_one
    grad_pair = jnp.stack([merge_heads(cross_grads[1]), merge_heads(cross_grads[2])], axis=2)
    grad_cross_kv = jnp.einsum(
        "cld,clkw->kwd", inputs, grad_pair, preferred_element_type=jnp.float32
    )
    bias_cross_v = jnp.sum(grad_pair[:, :, 1].astype(jnp.float32), axis=(0, 1))
    arrived = lax.all_to_all(grad_pair, "head", split_axis=1, concat_axis=3, tiled=True)
    grad_share = jnp.einsum(
        "clkw,kwd->cld", arrived, weights_whole, preferred_element_type=jnp.float32
    )
    own_start = head_index * rows_here
    own_mean = lax.dynamic_slice_in_dim(row_mean, own_start, rows_here, 1)
    own_inverse = lax.dynamic_slice_in_dim(inverse, own_start, rows_here, 1)
    standard = (tokens.astype(jnp.float32) - own_mean) * own_inverse
    scaled = grad_share * norm_gain[0]
    mean_plain = jnp.mean(scaled, axis=-1, keepdims=True)
    mean_cross = jnp.mean(scaled * standard, axis=-1, keepdims=True)
    grad_tokens = (own_inverse * (scaled - mean_plain - standard * mean_cross)).astype(jnp.bfloat16)
    gain_zero, shift_zero = lax.psum(
        (jnp.sum(grad_share * standard, axis=(0, 1)), jnp.sum(grad_share, axis=(0, 1))), "head"
    )
    grad_head_bias = jnp.stack(
        [jnp.stack([bias_cross_q, bias_cross_v]), jnp.stack([bias_self_q, bias_self_v])]
    )
    grad_up_bias = jnp.stack([upbias_cross, upbias_self])
    out_full = jnp.stack(
        [jnp.stack([bias_cross_attn, bias_cross_mlp]), jnp.stack([bias_self_attn, bias_self_mlp])]
    )
    grad_out_bias = share_of(out_full, head_index, head_width)
    grad_norm_gain = share_of(
        jnp.stack([gain_zero, gain_one, gain_two, gain_three, gain_four]), head_index, head_width
    )
    grad_norm_bias = share_of(
        jnp.stack([shift_zero, shift_one, shift_two, shift_three, shift_four]),
        head_index,
        head_width,
    )
    small_sums = lax.psum(
        (grad_head_bias, grad_up_bias, grad_out_bias, grad_norm_gain, grad_norm_bias), "dp"
    )
    combined = (
        lax.psum_scatter(grad_cross_q, "dp", scatter_dimension=1, tiled=True),
        lax.psum_scatter(grad_cross_kv, "dp", scatter_dimension=2, tiled=True),
        lax.psum_scatter(grad_cross_out, "dp", scatter_dimension=1, tiled=True),
        lax.psum_scatter(grad_cross_up, "dp", scatter_dimension=0, tiled=True),
        lax.psum_scatter(grad_cross_down, "dp", scatter_dimension=1, tiled=True),
        lax.psum_scatter(grad_self_qkv, "dp", scatter_dimension=2, tiled=True),
        lax.psum_scatter(grad_self_out, "dp", scatter_dimension=1, tiled=True),
        lax.psum_scatter(grad_self_up, "dp", scatter_dimension=0, tiled=True),
        lax.psum_scatter(grad_self_down, "dp", scatter_dimension=1, tiled=True),
    )
    cross_sums = combined[:5]
    self_sums = combined[5:]
    return (
        latents_out,
        grad_tokens,
        grad_latents,
        cross_sums[0],
        cross_sums[1],
        cross_sums[2],
        cross_sums[3],
        cross_sums[4],
        self_sums[0],
        self_sums[1],
        self_sums[2],
        self_sums[3],
        small_sums[0],
        small_sums[1],
        small_sums[2],
        small_sums[3],
        small_sums[4],
    )


def solution(mesh):
    in_specs = (
        P("dp", "head", None),
        P("dp"),
        P("dp", None),
        P("dp", None, None),
        P("head", None),
        P(None, "head", None),
        P("head", None),
        P(None, "head"),
        P("head", None),
        P(None, "head", None),
        P("head", None),
        P(None, "head"),
        P("head", None),
        P(None, None, "head"),
        P(None, "head"),
        P(),
        P(),
        P(),
        P("dp", None, None),
    )
    out_specs = (
        P("dp", None, None),
        P("dp", "head", None),
        P("dp", None, None),
        P("head", "dp"),
        P(None, "head", "dp"),
        P("head", "dp"),
        P("dp", "head"),
        P("head", "dp"),
        P(None, "head", "dp"),
        P("head", "dp"),
        P("dp", "head"),
        P("head", "dp"),
        P(None, None, "head"),
        P(None, "head"),
        P(None, None, "head"),
        P(None, "head"),
        P(None, "head"),
    )
    return jax.shard_map(local, mesh=mesh, in_specs=in_specs, out_specs=out_specs, check_vma=False)
```

profile of v0, /device:TPU:0, one launch (start us, length us, event | category | flops | bytes accessed | tf_op | source)
XLA Modules:
  0.0 1166.3 jit_solution(2360226538765348507)
XLA Ops:
  7.3 18.4 %copy.55 = bf16[1,1578,768]{2,0,1:T(2,128)(2,1)} copy(bf16[1,1578,768]{2,1,0:T(8,128)(2,1)} %param.19) | data formatting | bytes 4847616 | tf_op args[0]
  28.8 122.7 %all-gather.3.cloned.1.call-done = bf16[1,6312,768]{2,0,1:T(2,128)(2,1)} async-done(((bf16[1,1578,768]{2,0,1:T(2,128)(2,1)}), bf16[1,6312,768]{2,0,1:T(2,128)(2,1)}) %all-gather.3.cloned.1.call-update) | async-done | bytes 9695248 | tf_op jit(solution)/shard_map/all_gather | solution.py:146
  151.5 7.5 convert_reduce_fusion
  159.0 14.1 %fusion.4 = f32[6312]{0:T(1024)S(1)} fusion(f32[6312]{0:T(1024)S(1)} %broadcast_multiply_fusion, bf16[1,6312,768]{2,0,1:T(2,128)(2,1)} %all-gather.3.cloned.1.call-done), kind=kLoop, calls=%fused_computation.6 | loop fusion | flops 19384152 | bytes 9745728 | tf_op jit(solution)/shard_map/reduce_sum | solution.py:152
  173.2 5.6 fusion.10
  178.9 4.1 convolution_bitcast_fusion
  185.2 3.1 convolution_select_fusion
  188.3 6.2 fusion.155
  194.5 5.0 fusion.34
  201.4 31.3 %all-reduce.12.cloned.1.call-done = bf16[1,128,768]{2,1,0:T(8,128)(2,1)} async-done(((bf16[1,128,768]{2,1,0:T(8,128)(2,1)}), bf16[1,128,768]{2,1,0:T(8,128)(2,1)}) %all-reduce.12.cloned.1.call-update) | async-done | bytes 196624 | tf_op jit(solution)/shard_map/psum | solution.py:36
  239.6 30.8 %all-reduce.14.cloned.1.call-done = bf16[1,128,768]{2,1,0:T(8,128)(2,1)} async-done(((bf16[1,128,768]{2,1,0:T(8,128)(2,1)}), bf16[1,128,768]{2,1,0:T(8,128)(2,1)}) %all-reduce.14.cloned.1.call-update) | async-done | bytes 196624 | tf_op jit(solution)/shard_map/psum | solution.py:36
  271.8 1.6 convolution_bitcast_fusion.5
  276.4 1.9 convolution_convert_fusion.13
  278.4 1.7 fusion.25
  280.2 32.1 %all-reduce.16.cloned.1.call-done = bf16[1,128,768]{2,1,0:T(8,128)(2,1)} async-done(((bf16[1,128,768]{2,1,0:T(8,128)(2,1)}), bf16[1,128,768]{2,1,0:T(8,128)(2,1)}) %all-reduce.16.cloned.1.call-update) | async-done | bytes 196624 | tf_op jit(solution)/shard_map/psum | solution.py:36
  316.0 2.6 convert_reduce_fusion.7
  320.6 32.1 %all-reduce.18.cloned.1.call-done = bf16[1,128,768]{2,1,0:T(8,128)(2,1)} async-done(((bf16[1,128,768]{2,1,0:T(8,128)(2,1)}), bf16[1,128,768]{2,1,0:T(8,128)(2,1)}) %all-reduce.18.cloned.1.call-update) | async-done | bytes 196624 | tf_op jit(solution)/shard_map/psum | solution.py:40
  352.7 1.7 convert_reduce_fusion.5
  355.2 1.8 fusion.78
  357.0 1.9 fusion.149
  360.1 1.9 convert_reduce_fusion.9
  366.9 2.2 fusion.23
  369.2 32.1 %all-reduce.20.cloned.1.call-done = bf16[1,128,768]{2,1,0:T(8,128)(2,1)} async-done(((bf16[1,128,768]{2,1,0:T(8,128)(2,1)}), bf16[1,128,768]{2,1,0:T(8,128)(2,1)}) %all-reduce.20.cloned.1.call-update) | async-done | bytes 196624 | tf_op jit(solution)/shard_map/psum | solution.py:40
  401.3 1.8 convert_reduce_fusion.4
  403.2 1.8 fusion.79
  405.0 1.7 fusion.151
  410.3 2.4 fusion.29
  412.8 29.3 %all-reduce.22.cloned.1.call-done = bf16[1,128,768]{2,1,0:T(8,128)(2,1)} async-done(((bf16[1,128,768]{2,1,0:T(8,128)(2,1)}), bf16[1,128,768]{2,1,0:T(8,128)(2,1)}) %all-reduce.22.cloned.1.call-update) | async-done | bytes 196624 | tf_op jit(solution)/shard_map/psum | solution.py:40
  447.5 11.8 %multiply_reduce_fusion = (f32[3,128]{1,0:T(4,128)S(1)}, f32[3,128,6312]{1,2,0:T(8,128)}) fusion(f32[3,128,6312]{1,2,0:T(8,128)} %get-tuple-element.188, f32[3,128]{1,0:T(4,128)S(1)} %copy-done.84, bf16[128,3,64]{0,2,1:T(8,128)(2,1)S(1)} %bitcast.256, f32[6312,3,64]{0,2,1:T(8,128)} %bitcast.227, f32[3,64]{1,0:T(4,128)S(1)} %copy-done.93), kind=kOutput, calls=%fused_computation.16 | convolution fusion | flops 319942272 | bytes 24291072 | tf_op jit(solution)/shard_map/while/body/eval_jaxpr/qhe,khe->hqk/dot_general | solution.py:67
  459.3 9.9 multiply_convert_fusion
  469.2 4.3 convert_reduce_fusion.11
  478.4 6.9 convert_reduce_fusion.1
  485.7 4.1 convolution_convert_fusion.1
  491.2 8.9 fusion.11
  500.1 3.5 copy.71
  503.7 3.3 reshape.768
  507.0 1.7 fusion.113
  508.7 4.2 copy.75
  513.0 4.7 reshape.772
  518.4 2.0 fusion.142
  520.4 1.9 fusion.99
  522.5 2.1 fusion.127
  524.6 5.1 pad_maximum_fusion
  529.6 16.4 %copy.61 = bf16[1,6312,2,192]{3,2,0,1:T(2,128)(2,1)} copy(bf16[1,6312,2,192]{1,3,2,0:T(8,128)(2,1)} %pad_maximum_fusion) | data formatting | bytes 9695232 | tf_op jit(solution)/shard_map/stack | solution.py:272
  546.1 5.3 all-to-all-start
  551.8 1.9 fusion.91
  558.5 2.1 add_add_fusion.4
  560.5 13.6 %reduce-scatter.36.cloned.1.call-done = f32[96,192]{1,0:T(8,128)} async-done(((f32[768,192]{1,0:T(8,128)}), f32[96,192]{1,0:T(8,128)}) %reduce-scatter.36.cloned.1.call-update) | async-done | bytes 73744
  574.1 1.6 copy.78
  575.7 63.7 %reduce-scatter.28.cloned.1.call-done = f32[96,192]{1,0:T(8,128)} async-done(((f32[768,192]{1,0:T(8,128)}), f32[96,192]{1,0:T(8,128)}) %reduce-scatter.28.cloned.1.call-update) | async-done | bytes 73744
  641.1 64.0 %reduce-scatter.32.cloned.1.call-done = f32[96,192]{1,0:T(8,128)} async-done(((f32[768,192]{1,0:T(8,128)}), f32[96,192]{1,0:T(8,128)}) %reduce-scatter.32.cloned.1.call-update) | async-done | bytes 73744
  706.7 65.4 %reduce-scatter.30.cloned.1.call-done = f32[96,384]{1,0:T(8,128)} async-done(((f32[768,384]{1,0:T(8,128)}), f32[96,384]{1,0:T(8,128)}) %reduce-scatter.30.cloned.1.call-update) | async-done | bytes 147472
  774.0 68.6 %reduce-scatter.34.cloned.1.call-done = f32[96,576]{1,0:T(8,128)} async-done(((f32[768,576]{1,0:T(8,128)}), f32[96,576]{1,0:T(8,128)}) %reduce-scatter.34.cloned.1.call-update) | async-done | bytes 221200
  844.6 17.2 %copy.62 = bf16[1,4,1578,2,192]{2,4,1,3,0:T(8,128)(2,1)} copy(bf16[1,4,1578,2,192]{4,3,2,1,0:T(2,128)(2,1)} %bitcast.46) | data formatting | bytes 9695232 | tf_op jit(solution)/shard_map/all_to_all | solution.py:277
  861.8 5.2 all-gather.5.cloned.1.call-done
  867.0 9.0 fusion.13
  876.1 2.2 copy-done.5
  878.9 6.4 all-reduce.2
  885.4 37.7 %all-reduce.1 = (f32[2,2,192]{2,1,0:T(2,128)}, f32[2,768]{1,0:T(2,128)}, f32[2,2,192]{2,1,0:T(2,128)}, f32[5,192]{1,0:T(8,128)}, f32[5,192]{1,0:T(8,128)}) all-reduce(f32[2,2,192]{2,1,0:T(2,128)S(1)} %pad_maximum_fusion.2, f32[2,768]{1,0:T(2,128)S(1)} %pad_maximum_fusion.1, ...), channel_id=1, replica_groups=mesh['dp'=8,'head'=4] {'dp'}, use_global_device_ids=true, to_apply=%region_47.48 | all-reduce | flops 4992 | bytes 39936 | tf_op jit(solution)/shard_map/psum | solution.py:308
  923.1 5.2 fusion.16
  928.4 12.5 %reduce-scatter.24.cloned.1.call-done = f32[96,768]{1,0:T(8,128)} async-done(((f32[768,768]{1,0:T(8,128)}), f32[96,768]{1,0:T(8,128)}) %reduce-scatter.24.cloned.1.call-update) | async-done | bytes 294928 | tf_op jit(solution)/shard_map/reduce_scatter | solution.py:319
  940.9 72.7 %reduce-scatter.26.cloned.1.call-done = f32[768,96]{0,1:T(8,128)} async-done(((f32[768,768]{0,1:T(8,128)}), f32[768,96]{0,1:T(8,128)}) %reduce-scatter.26.cloned.1.call-update) | async-done | bytes 294928 | tf_op jit(solution)/shard_map/reduce_scatter | solution.py:320
  1013.6 72.9 %reduce-scatter.20.cloned.1.call-done = f32[96,768]{1,0:T(8,128)} async-done(((f32[768,768]{1,0:T(8,128)}), f32[96,768]{1,0:T(8,128)}) %reduce-scatter.20.cloned.1.call-update) | async-done | bytes 294928 | tf_op jit(solution)/shard_map/reduce_scatter | solution.py:315
  1086.5 72.8 %reduce-scatter.22.cloned.1.call-done = f32[768,96]{0,1:T(8,128)} async-done(((f32[768,768]{0,1:T(8,128)}), f32[768,96]{0,1:T(8,128)}) %reduce-scatter.22.cloned.1.call-update) | async-done | bytes 294928 | tf_op jit(solution)/shard_map/reduce_scatter | solution.py:316
  (341 shorter events, 59.1 us)
Async XLA Ops:
  7.2 229.9 %copy-start = (bf16[768,768]{1,0:T(8,128)(2,1)S(1)}, bf16[768,768]{1,0:T(8,128)(2,1)}, u32[]{:S(2)}) copy-start(bf16[768,768]{1,0:T(8,128)(2,1)} %param.27) | copy-start | bytes 3538948
  7.2 18.6 %copy-start.90 = (f32[2,2,192]{2,1,0:T(2,128)S(1)}, f32[2,2,192]{2,1,0:T(2,128)}, u32[]{:S(2)}) copy-start(f32[2,2,192]{2,1,0:T(2,128)} %param.32) | copy-start | bytes 9220
  7.2 19.3 %copy-start.100 = (s32[1,40]{1,0:T(1,128)S(1)}, s32[1,40]{1,0:T(1,128)}, u32[]{:S(2)}) copy-start(s32[1,40]{1,0:T(1,128)} %param.21) | copy-start | bytes 484
  7.2 19.4 %copy-start.72 = (f32[2,2,768]{2,1,0:T(2,128)S(1)}, f32[2,2,768]{2,1,0:T(2,128)}, u32[]{:S(2)}) copy-start(f32[2,2,768]{2,1,0:T(2,128)} %param.34) | copy-start | bytes 36868
  7.2 20.1 %copy-start.73 = (f32[5,768]{1,0:T(8,128)S(1)}, f32[5,768]{1,0:T(8,128)}, u32[]{:S(2)}) copy-start(f32[5,768]{1,0:T(8,128)} %param.36) | copy-start | bytes 46084
  7.2 20.7 %copy-start.74 = (f32[5,768]{1,0:T(8,128)S(1)}, f32[5,768]{1,0:T(8,128)}, u32[]{:S(2)}) copy-start(f32[5,768]{1,0:T(8,128)} %param.35) | copy-start | bytes 46084
  7.3 20.7 %copy-start.3 = (bf16[1,128,768]{2,1,0:T(8,128)(2,1)S(1)}, bf16[1,128,768]{2,1,0:T(8,128)(2,1)}, u32[]{:S(2)}) copy-start(bf16[1,128,768]{2,1,0:T(8,128)(2,1)} %param.22) | copy-start | bytes 589828
  7.3 21.1 %copy-start.33 = (bf16[192,768]{1,0:T(8,128)(2,1)S(1)}, bf16[192,768]{1,0:T(8,128)(2,1)}, u32[]{:S(2)}) copy-start(bf16[192,768]{1,0:T(8,128)(2,1)} %param.23) | copy-start | bytes 884740
  7.3 144.2 %all-gather.3.cloned.1.call-start = ((), (), s32[]{:S(2)}) async-start(), calls=%async_computation.10 | async-start | bytes 24238080 | tf_op jit(solution)/shard_map/all_gather | solution.py:146
  25.7 207.0 %all-reduce.12.cloned.1.call-start = ((), (), s32[]{:S(2)}) async-start(), calls=%async_computation.11 | async-start | bytes 393216 | tf_op jit(solution)/shard_map/psum | solution.py:36
  25.9 168.6 %copy-start.92 = (f32[3,64]{1,0:T(4,128)}, f32[3,64]{1,0:T(4,128)S(1)}, u32[]{:S(2)}) copy-start(f32[3,64]{1,0:T(4,128)S(1)} %add.344) | copy-start | bytes 2308
  27.9 131.0 %copy-start.60 = (f32[768]{0:T(1024)}, f32[768]{0:T(1024)S(1)}, u32[]{:S(2)}) copy-start(f32[768]{0:T(1024)S(1)} %get-tuple-element.152) | copy-start | bytes 9220
  27.9 207.1 %copy-start.47 = (f32[768]{0:T(1024)}, f32[768]{0:T(1024)S(1)}, u32[]{:S(2)}) copy-start(f32[768]{0:T(1024)S(1)} %get-tuple-element.151) | copy-start | bytes 9220
  28.0 130.9 %copy-start.43 = (f32[768]{0:T(1024)}, f32[768]{0:T(1024)S(1)}, u32[]{:S(2)}) copy-start(f32[768]{0:T(1024)S(1)} %get-tuple-element.147) | copy-start | bytes 9220
  28.0 145.1 %copy-start.45 = (f32[768]{0:T(1024)}, f32[768]{0:T(1024)S(1)}, u32[]{:S(2)}) copy-start(f32[768]{0:T(1024)S(1)} %get-tuple-element.148) | copy-start | bytes 9220
  28.1 130.8 %copy-start.70 = (f32[128]{0:T(128)}, f32[128]{0:T(128)S(1)}, u32[]{:S(2)}) copy-start(f32[128]{0:T(128)S(1)} %broadcast_multiply_fusion.6) | copy-start | bytes 1540
  28.3 130.6 %copy-start.94 = (f32[128]{0:T(128)}, f32[128]{0:T(128)S(1)}, u32[]{:S(2)}) copy-start(f32[128]{0:T(128)S(1)} %fusion.75) | copy-start | bytes 1540
  28.4 130.6 %copy-start.86 = (f32[128]{0:T(128)}, f32[128]{0:T(128)S(1)}, u32[]{:S(2)}) copy-start(f32[128]{0:T(128)S(1)} %fusion.120) | copy-start | bytes 1540
  28.7 154.8 %copy-start.35 = (bf16[128,192]{0,1:T(8,128)(2,1)}, bf16[128,192]{0,1:T(8,128)(2,1)S(1)}, u32[]{:S(2)}) copy-start(bf16[128,192]{0,1:T(8,128)(2,1)S(1)} %fusion.33) | copy-start | bytes 147460
  159.0 14.2 %copy-start.32 = (f32[6312]{0:T(1024)}, f32[6312]{0:T(1024)S(1)}, u32[]{:S(2)}) copy-start(f32[6312]{0:T(1024)S(1)} %broadcast_multiply_fusion) | copy-start | bytes 75748
  159.0 14.2 %copy-start.2 = (bf16[1,6312,768]{2,0,1:T(2,128)(2,1)S(1)}, bf16[1,6312,768]{2,0,1:T(2,128)(2,1)}, u32[]{:S(2)}) copy-start(bf16[1,6312,768]{2,0,1:T(2,128)(2,1)} %all-gather.3.cloned.1.call-done) | copy-start | bytes 29085700
  183.3 11.2 copy-start.9
  194.5 40.5 %copy-start.11 = (bf16[768,768]{1,0:T(8,128)(2,1)S(1)}, bf16[768,768]{1,0:T(8,128)(2,1)}, u32[]{:S(2)}) copy-start(bf16[768,768]{1,0:T(8,128)(2,1)} %param.26) | copy-start | bytes 3538948
  199.6 70.8 %copy-start.37 = (bf16[3,64,128]{2,1,0:T(8,128)(2,1)}, bf16[3,64,128]{2,1,0:T(8,128)(2,1)S(1)}, u32[]{:S(2)}) copy-start(bf16[3,64,128]{2,1,0:T(8,128)(2,1)S(1)} %fusion.34) | copy-start | bytes 147460
  199.6 70.8 %copy-start.62 = (f32[768]{0:T(1024)S(1)}, f32[768]{0:T(1024)}, u32[]{:S(2)}) copy-start(f32[768]{0:T(1024)} %get-tuple-element.156) | copy-start | bytes 9220
  199.6 72.2 %copy-start.50 = (f32[768]{0:T(1024)S(1)}, f32[768]{0:T(1024)}, u32[]{:S(2)}) copy-start(f32[768]{0:T(1024)} %get-tuple-element.154) | copy-start | bytes 9220
  200.6 69.8 %all-reduce.14.cloned.1.call-start = ((), (), s32[]{:S(2)}) async-start(), calls=%async_computation.12 | async-start | bytes 393216 | tf_op jit(solution)/shard_map/psum | solution.py:36
  232.7 37.7 %copy-start.6 = (bf16[1,128,768]{2,1,0:T(8,128)(2,1)S(1)}, bf16[1,128,768]{2,1,0:T(8,128)(2,1)}, u32[]{:S(2)}) copy-start(bf16[1,128,768]{2,1,0:T(8,128)(2,1)} %all-reduce.12.cloned.1.call-done) | copy-start | bytes 589828
  232.7 45.7 %copy-start.19 = (bf16[192,768]{1,0:T(8,128)(2,1)S(1)}, bf16[192,768]{1,0:T(8,128)(2,1)}, u32[]{:S(2)}) copy-start(bf16[192,768]{1,0:T(8,128)(2,1)} %param.29) | copy-start | bytes 884740
  233.9 36.5 %copy-start.52 = (f32[128]{0:T(128)}, f32[128]{0:T(128)S(1)}, u32[]{:S(2)}) copy-start(f32[128]{0:T(128)S(1)} %broadcast_multiply_fusion.5) | copy-start | bytes 1540
  235.0 35.4 %copy-start.96 = (f32[128]{0:T(128)}, f32[128]{0:T(128)S(1)}, u32[]{:S(2)}) copy-start(f32[128]{0:T(128)S(1)} %multiply_reduce_fusion.3) | copy-start | bytes 1540
  235.0 35.4 %copy-start.76 = (f32[128]{0:T(128)}, f32[128]{0:T(128)S(1)}, u32[]{:S(2)}) copy-start(f32[128]{0:T(128)S(1)} %fusion.121) | copy-start | bytes 1540
  237.1 77.1 %copy-start.10 = (bf16[768,768]{1,0:T(8,128)(2,1)S(1)}, bf16[768,768]{1,0:T(8,128)(2,1)}, u32[]{:S(2)}) copy-start(bf16[768,768]{1,0:T(8,128)(2,1)} %param.30) | copy-start | bytes 3538948
  238.2 74.1 %all-reduce.16.cloned.1.call-start = ((), (), s32[]{:S(2)}) async-start(), calls=%async_computation.13 | async-start | bytes 393216 | tf_op jit(solution)/shard_map/psum | solution.py:36
  274.1 38.2 %copy-start.30 = (bf16[1,128,1,192]{1,3,2,0:T(8,128)(2,1)}, bf16[1,128,1,192]{1,3,2,0:T(8,128)(2,1)S(1)}, u32[]{:S(2)}) copy-start(bf16[1,128,1,192]{1,3,2,0:T(8,128)(2,1)S(1)} %slice.134) | copy-start | bytes 147460
  274.9 37.4 %copy-start.31 = (bf16[128,3,64]{0,2,1:T(8,128)(2,1)}, bf16[128,3,64]{0,2,1:T(8,128)(2,1)S(1)}, u32[]{:S(2)}) copy-start(bf16[128,3,64]{0,2,1:T(8,128)(2,1)S(1)} %multiply_convert_fusion.4) | copy-start | bytes 147460
  280.1 72.6 %all-reduce.18.cloned.1.call-start = ((), (), s32[]{:S(2)}) async-start(), calls=%async_computation.14 | async-start | bytes 393216 | tf_op jit(solution)/shard_map/psum | solution.py:40
  320.5 82.6 %copy-start.98 = (f32[128]{0:T(128)S(1)}, f32[128]{0:T(128)}, u32[]{:S(2)}) copy-start(f32[128]{0:T(128)} %copy-done.97) | copy-start | bytes 1540
  320.5 82.6 %copy-start.55 = (f32[128]{0:T(128)S(1)}, f32[128]{0:T(128)}, u32[]{:S(2)}) copy-start(f32[128]{0:T(128)} %copy-done.54) | copy-start | bytes 1540
  320.5 82.6 %copy-start.79 = (f32[128]{0:T(128)S(1)}, f32[128]{0:T(128)}, u32[]{:S(2)}) copy-start(f32[128]{0:T(128)} %copy-done.78) | copy-start | bytes 1540
  320.6 80.8 %all-reduce.20.cloned.1.call-start = ((), (), s32[]{:S(2)}) async-start(), calls=%async_computation.15 | async-start | bytes 393216 | tf_op jit(solution)/shard_map/psum | solution.py:40
  354.5 52.2 %copy-start.15 = (f32[128,768]{1,0:T(8,128)S(1)}, f32[128,768]{1,0:T(8,128)}, u32[]{:S(2)}) copy-start(f32[128,768]{1,0:T(8,128)} %copy-done.14) | copy-start | bytes 1179652
  362.0 43.0 %copy-start.40 = (bf16[3,64,128]{2,1,0:T(8,128)(2,1)}, bf16[3,64,128]{2,1,0:T(8,128)(2,1)S(1)}, u32[]{:S(2)}) copy-start(bf16[3,64,128]{2,1,0:T(8,128)(2,1)S(1)} %get-tuple-element.197) | copy-start | bytes 147460
  365.3 39.7 %copy-start.26 = (bf16[3,64,128]{2,1,0:T(8,128)(2,1)}, bf16[3,64,128]{2,1,0:T(8,128)(2,1)S(1)}, u32[]{:S(2)}) copy-start(bf16[3,64,128]{2,1,0:T(8,128)(2,1)S(1)} %convolution_convert_fusion.11) | copy-start | bytes 147460
  366.9 38.1 %copy-start.28 = (bf16[3,64,128]{2,1,0:T(8,128)(2,1)}, bf16[3,64,128]{2,1,0:T(8,128)(2,1)S(1)}, u32[]{:S(2)}) copy-start(bf16[3,64,128]{2,1,0:T(8,128)(2,1)S(1)} %get-tuple-element.199) | copy-start | bytes 147460
  369.1 72.9 %all-reduce.22.cloned.1.call-start = ((), (), s32[]{:S(2)}) async-start(), calls=%async_computation.16 | async-start | bytes 393216 | tf_op jit(solution)/shard_map/psum | solution.py:40
  401.3 7.3 copy-start.12
  407.9 39.5 %copy-start.84 = (f32[3,128]{1,0:T(4,128)S(1)}, f32[3,128]{1,0:T(4,128)}, u32[]{:S(2)}) copy-start(f32[3,128]{1,0:T(4,128)} %copy-done.83) | copy-start | bytes 4612
  407.9 39.5 %copy-start.93 = (f32[3,64]{1,0:T(4,128)S(1)}, f32[3,64]{1,0:T(4,128)}, u32[]{:S(2)}) copy-start(f32[3,64]{1,0:T(4,128)} %copy-done.92) | copy-start | bytes 2308
  409.9 146.2 %all-reduce.24.cloned.1.call-start = ((), (), s32[]{:S(2)}) async-start(), calls=%async_computation.27 | async-start | bytes 786432 | tf_op jit(solution)/shard_map/psum | solution.py:36
  469.2 7.9 copy-start.38
  474.5 99.6 %reduce-scatter.36.cloned.1.call-start = ((), (), s32[]{:S(2)}) async-start(), calls=%async_computation.26 | async-start | bytes 884736
  475.8 163.7 %reduce-scatter.28.cloned.1.call-start = ((), (), s32[]{:S(2)}) async-start(), calls=%async_computation.22 | async-start | bytes 884736
  478.4 226.7 %reduce-scatter.32.cloned.1.call-start = ((), (), s32[]{:S(2)}) async-start(), calls=%async_computation.24 | async-start | bytes 884736
  485.4 286.7 %reduce-scatter.30.cloned.1.call-start = ((), (), s32[]{:S(2)}) async-start(), calls=%async_computation.23 | async-start | bytes 1327104
  506.9 335.6 %reduce-scatter.34.cloned.1.call-start = ((), (), s32[]{:S(2)}) async-start(), calls=%async_computation.25 | async-start | bytes 2211840
  517.7 349.4 %all-gather.5.cloned.1.call-start = ((), (), s32[]{:S(2)}) async-start(), calls=%async_computation.17 | async-start | bytes 2949120 | tf_op jit(solution)/shard_map/all_gather | solution.py:147
  518.3 422.6 %reduce-scatter.24.cloned.1.call-start = ((), (), s32[]{:S(2)}) async-start(), calls=%async_computation.20 | async-start | bytes 2654208 | tf_op jit(solution)/shard_map/reduce_scatter | solution.py:319
  520.4 493.2 %reduce-scatter.26.cloned.1.call-start = ((), (), s32[]{:S(2)}) async-start(), calls=%async_computation.21 | async-start | bytes 2654208 | tf_op jit(solution)/shard_map/reduce_scatter | solution.py:320
  522.4 564.1 %reduce-scatter.20.cloned.1.call-start = ((), (), s32[]{:S(2)}) async-start(), calls=%async_computation.18 | async-start | bytes 2654208 | tf_op jit(solution)/shard_map/reduce_scatter | solution.py:315
  546.1 298.5 %all-to-all-start = ((bf16[1,6312,2,192]{3,2,0,1:T(2,128)(2,1)}), bf16[1,6312,2,192]{3,2,0,1:T(2,128)(2,1)}, u32[]{:S(2)}, u32[]{:S(2)}) async-start(bf16[1,6312,2,192]{3,2,0,1:T(2,128)(2,1)} %copy.61), calls=%async_computation | async-start | bytes 12926976 | tf_op jit(solution)/shard_map/all_to_all | solution.py:277
  551.5 607.7 %reduce-scatter.22.cloned.1.call-start = ((), (), s32[]{:S(2)}) async-start(), calls=%async_computation.19 | async-start | bytes 2654208 | tf_op jit(solution)/shard_map/reduce_scatter | solution.py:316
  844.6 22.4 %copy-start.46 = (f32[768]{0:T(1024)S(1)}, f32[768]{0:T(1024)}, u32[]{:S(2)}) copy-start(f32[768]{0:T(1024)} %copy-done.45) | copy-start | bytes 9220
  923.1 236.1 %copy-start.1 = (bf16[768,768]{1,0:T(8,128)(2,1)S(1)}, bf16[768,768]{1,0:T(8,128)(2,1)}, u32[]{:S(2)}) copy-start(bf16[768,768]{1,0:T(8,128)(2,1)} %param.27) | copy-start | bytes 3538948
  (56 other events, 239.0 us)
Sparse Core Ops, SparseCore 0:
  25.9 125.5 all-gather.2
  200.7 31.9 all-reduce.11
  238.3 32.0 all-reduce.13
  280.2 32.0 all-reduce.15
  320.7 32.0 all-reduce.17
  369.2 32.0 all-reduce.19
  410.0 32.0 all-reduce.21
  474.6 32.8 all-reduce.23
  510.8 63.2 reduce-scatter.35
  577.3 62.1 reduce-scatter.27
  642.8 62.2 reduce-scatter.31
  708.3 63.7 reduce-scatter.29
  776.1 66.3 reduce-scatter.33
  844.0 22.9 all-gather.4
  870.9 69.9 reduce-scatter.23
  944.8 68.7 reduce-scatter.25
  1017.5 68.9 reduce-scatter.19
  1090.4 68.7 reduce-scatter.21
where the time goes:
time: 1170 us
  waiting for transfers between devices  823 us (70%)
  matrix products  102 us (9%)
  local copies, waits for them, and re-layouts  92.2 us (8%)
  other arithmetic  81.6 us (7%)
  blocking collectives  44.1 us (4%)
  between operations  16.7 us (1%)
    unnamed x23, waiting for transfers between devices  276 us
    all_gather x1, waiting for transfers between devices, local(): lax.all_gather(tokens, 'head', axis=1, tiled=True)  123 us
    psum x4, waiting for transfers between devices, join_heads(): lax.psum(partial_sum.astype(jnp.bfloat16), 'head').astype(jnp.float32)  94.2 us
    psum x3, waiting for transfers between devices, join_back(): lax.psum(partial_sum.astype(jnp.bfloat16), 'head').astype(jnp.float32)  93.6 us
    reduce_scatter x1, waiting for transfers between devices, local(): lax.psum_scatter(grad_cross_up, 'dp', scatter_dimension=0, tiled=True)  72.9 us
    reduce_scatter x1, waiting for transfers between devices, local(): lax.psum_scatter(grad_cross_down, 'dp', scatter_dimension=1, tiled=True)  72.8 us
    reduce_scatter x1, waiting for transfers between devices, local(): lax.psum_scatter(grad_self_down, 'dp', scatter_dimension=1, tiled=True)  72.7 us
    unnamed x214, local copies, waits for them, and re-layouts  51.9 us
  transfers between devices with their start and end apart: 19, of which 17 were waited for; matrix products, arithmetic and copies ran while one was open for 11% of the time, Pallas kernels for 0%

commit v1 on v0

--- a/solution.py
+++ b/solution.py
@@ -9,6 +9,27 @@
 F_MAX = 16
 EPSILON = 1e-05
 NEGATIVE = -1e30
+
+
+def ring_gather(x, axis, dim):
+    count, here, rows = (lax.axis_size(axis), lax.axis_index(axis), x.shape[dim])
+    right = [(i, (i + 1) % count) for i in range(count)]
+    left = [(i, (i - 1) % count) for i in range(count)]
+    out = jnp.zeros((*x.shape[:dim], count * rows, *x.shape[dim + 1 :]), x.dtype)
+    out = lax.dynamic_update_slice_in_dim(out, x, here * rows, axis=dim)
+    from_left = from_right = x
+    halfway = count // 2
+    for turn in range(1, halfway + 1):
+        from_left = lax.ppermute(from_left, axis, right)
+        out = lax.dynamic_update_slice_in_dim(
+            out, from_left, (here - turn) % count * rows, axis=dim
+        )
+        if turn < count - halfway:
+            from_right = lax.ppermute(from_right, axis, left)
+            out = lax.dynamic_update_slice_in_dim(
+                out, from_right, (here + turn) % count * rows, axis=dim
+            )
+    return out
 
 
 def normed(tensor, gain_row, shift_row):
@@ -143,7 +164,7 @@
     )
     usable = (position[None, :] < frames[:, None] * P_SIZE) | (text_full == 1)
     gathered, weights_whole = (
-        lax.all_gather(tokens, "head", axis=1, tiled=True),
+        ring_gather(tokens, "head", 1),
         lax.all_gather(cross_kv, "head", axis=1, tiled=True),
     )
     full_rows = gathered.astype(jnp.float32)

time: 1170 us -> 1130 us (0.966)
  waiting for transfers between devices: 823 us -> 751 us
  local copies, waits for them, and re-layouts: 92.2 us -> 128 us
  other arithmetic: 81.6 us -> 64.9 us
    all_gather x1 -> x0, waiting for transfers between devices: 123 us -> none  [local(): lax.all_gather(tokens, 'head', axis=1, tiled=True)]
    ppermute x0 -> x3, waiting for transfers between devices: none -> 51 us  [the longest x2 51 us: ring_gather(): from_left = lax.ppermute(from_left, axis, right)]
    dynamic_update_slice x0 -> x4, local copies, waits for them, and re-layouts: none -> 50 us  [the longest x2 24.7 us: ring_gather(): lax.dynamic_update_slice_in_dim(out, from_left, (here - turn) % count * r...]
    unnamed x214 -> x215, local copies, waits for them, and re-layouts: 51.9 us -> 33.9 us
    unnamed x23 -> x22, waiting for transfers between devices: 276 us -> 274 us
  transfers between devices with their start and end apart: 19 -> 21, of which waited for: 17 -> 17; matrix products, arithmetic and copies ran while one was open for 11% -> 15% of each run, Pallas kernels for 0% -> 0%
where the time goes in v1:
time: 1130 us; the launch traced here: 1120 us
  waiting for transfers between devices  751 us (66%)
  local copies, waits for them, and re-layouts  128 us (11%)
  matrix products  108 us (10%)
  other arithmetic  64.9 us (6%)
  blocking collectives  44.2 us (4%)
  between operations  16.3 us (1%)
  starting transfers between devices  12 us (1%)
    unnamed x22, waiting for transfers between devices  274 us
    psum x4, waiting for transfers between devices, join_heads(): lax.psum(partial_sum.astype(jnp.bfloat16), 'head').astype(jnp.float32)  95.9 us
    psum x3, waiting for transfers between devices, join_back(): lax.psum(partial_sum.astype(jnp.bfloat16), 'head').astype(jnp.float32)  93.6 us
    reduce_scatter x1, waiting for transfers between devices, local(): lax.psum_scatter(grad_cross_up, 'dp', scatter_dimension=0, tiled=True)  73 us
    reduce_scatter x1, waiting for transfers between devices, local(): lax.psum_scatter(grad_cross_down, 'dp', scatter_dimension=1, tiled=True)  72.9 us
    reduce_scatter x1, waiting for transfers between devices, local(): lax.psum_scatter(grad_self_down, 'dp', scatter_dimension=1, tiled=True)  72.9 us
    ppermute x2, waiting for transfers between devices, ring_gather(): from_left = lax.ppermute(from_left, axis, right)  51 us
    psum x1, blocking collectives, local(): lax.psum((grad_head_bias, grad_up_bias, grad_out_bias, grad_norm_gain, gr...  37.9 us
  transfers between devices with their start and end apart: 21, of which 17 were waited for; matrix products, arithmetic and copies ran while one was open for 15% of the time, Pallas kernels for 0%

profile of v1, /device:TPU:0, one launch (start us, length us, event | category | flops | bytes accessed | tf_op | source)
XLA Modules:
  0.0 1123.8 jit_solution(12260332321112959065)
XLA Ops:
  7.8 2.0 collective-permute-start.1
  9.8 51.0 %collective-permute-done = bf16[1,1578,768]{2,1,0:T(8,128)(2,1)} collective-permute-done((bf16[1,1578,768]{2,1,0:T(8,128)(2,1)}, bf16[1,1578,768]{2,1,0:T(8,128)(2,1)}, u32[]{:S(2)}, u32[]{:S(2)}) %collective-permute-start) | collective-permute-done | bytes 2423840 | tf_op jit(solution)/shard_map/ppermute | solution.py:23
  60.8 2.4 collective-permute-start.2
  64.8 4.3 broadcast_in_dim.155
  69.2 12.7 %dynamic_update_slice.39 = bf16[1,6312,768]{2,1,0:T(8,128)(2,1)} dynamic-update-slice(bf16[1,6312,768]{2,1,0:T(8,128)(2,1)} %broadcast_in_dim.155, bf16[1,1578,768]{2,1,0:T(8,128)(2,1)} %param.19, s32[]{:T(128)} %constant.158.clone.1, s32[]{:T(128)S(6)} %select_n.46, s32[]{:T(128)} %constant.158.clone.1) | dynamic-update-slice | bytes 4847620 | tf_op jit(solution)/shard_map/dynamic_update_slice | solution.py:19
  84.1 12.1 %dynamic_update_slice.40 = bf16[1,6312,768]{2,1,0:T(8,128)(2,1)} dynamic-update-slice(bf16[1,6312,768]{2,1,0:T(8,128)(2,1)} %dynamic_update_slice.39, bf16[1,1578,768]{2,1,0:T(8,128)(2,1)} %collective-permute-done, s32[]{:T(128)} %constant.158.clone.1, s32[]{:T(128)S(6)} %select_n.48, s32[]{:T(128)} %constant.158.clone.1) | dynamic-update-slice | bytes 4847620 | tf_op jit(solution)/shard_map/dynamic_update_slice | solution.py:24
  96.1 12.6 %dynamic_update_slice.41 = bf16[1,6312,768]{2,1,0:T(8,128)(2,1)} dynamic-update-slice(bf16[1,6312,768]{2,1,0:T(8,128)(2,1)} %dynamic_update_slice.40, bf16[1,1578,768]{2,1,0:T(8,128)(2,1)} %collective-permute-done.1, s32[]{:T(128)} %constant.158.clone.1, s32[]{:T(128)S(6)} %select_n.50, s32[]{:T(128)} %constant.158.clone.1) | dynamic-update-slice | bytes 4847620 | tf_op jit(solution)/shard_map/dynamic_update_slice | solution.py:29
  108.7 12.6 %dynamic_update_slice.42 = bf16[1,6312,768]{2,1,0:T(8,128)(2,1)} dynamic-update-slice(bf16[1,6312,768]{2,1,0:T(8,128)(2,1)} %dynamic_update_slice.41, bf16[1,1578,768]{2,1,0:T(8,128)(2,1)} %collective-permute-done.2, s32[]{:T(128)} %constant.158.clone.1, s32[]{:T(128)S(6)} %select_n.52, s32[]{:T(128)} %constant.158.clone.1) | dynamic-update-slice | bytes 4847620 | tf_op jit(solution)/shard_map/dynamic_update_slice | solution.py:24
  121.4 5.3 convert_reduce_fusion
  127.9 5.2 fusion.4
  133.7 4.4 convolution_bitcast_fusion
  140.4 3.1 convolution_select_fusion
  143.5 6.3 fusion.157
  149.8 5.0 fusion.34
  156.7 33.0 %all-reduce.12.cloned.1.call-done = bf16[1,128,768]{2,1,0:T(8,128)(2,1)} async-done(((bf16[1,128,768]{2,1,0:T(8,128)(2,1)}), bf16[1,128,768]{2,1,0:T(8,128)(2,1)}) %all-reduce.12.cloned.1.call-update) | async-done | bytes 196624 | tf_op jit(solution)/shard_map/psum | solution.py:57
  196.5 30.8 %all-reduce.14.cloned.1.call-done = bf16[1,128,768]{2,1,0:T(8,128)(2,1)} async-done(((bf16[1,128,768]{2,1,0:T(8,128)(2,1)}), bf16[1,128,768]{2,1,0:T(8,128)(2,1)}) %all-reduce.14.cloned.1.call-update) | async-done | bytes 196624 | tf_op jit(solution)/shard_map/psum | solution.py:57
  233.3 1.9 convolution_convert_fusion.13
  237.1 32.1 %all-reduce.16.cloned.1.call-done = bf16[1,128,768]{2,1,0:T(8,128)(2,1)} async-done(((bf16[1,128,768]{2,1,0:T(8,128)(2,1)}), bf16[1,128,768]{2,1,0:T(8,128)(2,1)}) %all-reduce.16.cloned.1.call-update) | async-done | bytes 196624 | tf_op jit(solution)/shard_map/psum | solution.py:57
  272.9 2.6 convert_reduce_fusion.7
  277.5 32.1 %all-reduce.18.cloned.1.call-done = bf16[1,128,768]{2,1,0:T(8,128)(2,1)} async-done(((bf16[1,128,768]{2,1,0:T(8,128)(2,1)}), bf16[1,128,768]{2,1,0:T(8,128)(2,1)}) %all-reduce.18.cloned.1.call-update) | async-done | bytes 196624 | tf_op jit(solution)/shard_map/psum | solution.py:61
  309.7 1.7 convert_reduce_fusion.5
  312.1 1.8 fusion.78
  313.9 1.9 fusion.151
  317.0 1.9 convert_reduce_fusion.9
  323.9 2.2 fusion.23
  326.1 32.1 %all-reduce.20.cloned.1.call-done = bf16[1,128,768]{2,1,0:T(8,128)(2,1)} async-done(((bf16[1,128,768]{2,1,0:T(8,128)(2,1)}), bf16[1,128,768]{2,1,0:T(8,128)(2,1)}) %all-reduce.20.cloned.1.call-update) | async-done | bytes 196624 | tf_op jit(solution)/shard_map/psum | solution.py:61
  358.3 1.8 convert_reduce_fusion.4
  360.1 1.8 fusion.79
  367.3 2.4 fusion.29
  369.7 29.3 %all-reduce.22.cloned.1.call-done = bf16[1,128,768]{2,1,0:T(8,128)(2,1)} async-done(((bf16[1,128,768]{2,1,0:T(8,128)(2,1)}), bf16[1,128,768]{2,1,0:T(8,128)(2,1)}) %all-reduce.22.cloned.1.call-update) | async-done | bytes 196624 | tf_op jit(solution)/shard_map/psum | solution.py:61
  404.4 11.8 %multiply_reduce_fusion = (f32[3,128]{1,0:T(4,128)S(1)}, f32[3,128,6312]{1,2,0:T(8,128)}) fusion(f32[3,128,6312]{1,2,0:T(8,128)} %get-tuple-element.188, f32[3,128]{1,0:T(4,128)S(1)} %copy-done.84, bf16[128,3,64]{0,2,1:T(8,128)(2,1)S(1)} %bitcast.256, f32[6312,3,64]{0,2,1:T(8,128)} %bitcast.227, f32[3,64]{1,0:T(4,128)S(1)} %copy-done.93), kind=kOutput, calls=%fused_computation.16 | convolution fusion | flops 319942272 | bytes 24291072 | tf_op jit(solution)/shard_map/while/body/eval_jaxpr/qhe,khe->hqk/dot_general | solution.py:88
  416.2 9.9 multiply_convert_fusion
  426.2 4.3 convert_reduce_fusion.11
  435.3 5.5 convolution_convert_fusion.1
  440.9 6.9 convert_reduce_fusion.1
  448.1 12.9 %fusion.11 = f32[2,192,768]{2,1,0:T(8,128)} fusion(bf16[1,6312,1,192]{1,3,2,0:T(8,128)(2,1)} %bitcast.228, bf16[1,6312,1,192]{1,3,2,0:T(8,128)(2,1)} %bitcast.222, bf16[1,6312,768]{2,1,0:T(8,128)(2,1)} %dynamic_update_slice.42, f32[768]{0:T(1024)S(1)} %copy-done.89, f32[768]{0:T(1024)S(1)} %copy-done.45, f32[6312]{0:T(1024)S(1)} %copy-done.43, ...), kind=kOutput, calls=%fused_computation.21 | convolution fusion | flops 3754478592 | bytes 15779136 | tf_op jit(solution)/shard_map/cld,clkw->kwd/dot_general | solution.py:294
  461.1 3.5 copy.61
  464.6 3.2 reshape.768
  469.6 4.2 copy.65
  473.8 4.7 reshape.772
  479.5 2.0 fusion.142
  481.5 1.9 fusion.99
  483.6 2.0 fusion.127
  485.6 5.1 pad_maximum_fusion
  490.7 16.4 %copy.51 = bf16[1,6312,2,192]{3,2,0,1:T(2,128)(2,1)} copy(bf16[1,6312,2,192]{1,3,2,0:T(8,128)(2,1)} %pad_maximum_fusion) | data formatting | bytes 9695232 | tf_op jit(solution)/shard_map/stack | solution.py:293
  507.2 5.3 all-to-all-start
  512.9 2.0 fusion.91
  518.2 2.1 add_add_fusion.4
  520.3 10.8 reduce-scatter.36.cloned.1.call-done
  532.7 64.0 %reduce-scatter.28.cloned.1.call-done = f32[96,192]{1,0:T(8,128)} async-done(((f32[768,192]{1,0:T(8,128)}), f32[96,192]{1,0:T(8,128)}) %reduce-scatter.28.cloned.1.call-update) | async-done | bytes 73744
  598.3 63.8 %reduce-scatter.32.cloned.1.call-done = f32[96,192]{1,0:T(8,128)} async-done(((f32[768,192]{1,0:T(8,128)}), f32[96,192]{1,0:T(8,128)}) %reduce-scatter.32.cloned.1.call-update) | async-done | bytes 73744
  663.8 65.6 %reduce-scatter.30.cloned.1.call-done = f32[96,384]{1,0:T(8,128)} async-done(((f32[768,384]{1,0:T(8,128)}), f32[96,384]{1,0:T(8,128)}) %reduce-scatter.30.cloned.1.call-update) | async-done | bytes 147472
  731.3 68.5 %reduce-scatter.34.cloned.1.call-done = f32[96,576]{1,0:T(8,128)} async-done(((f32[768,576]{1,0:T(8,128)}), f32[96,576]{1,0:T(8,128)}) %reduce-scatter.34.cloned.1.call-update) | async-done | bytes 221200
  801.8 17.3 %copy.52 = bf16[1,4,1578,2,192]{2,4,1,3,0:T(8,128)(2,1)} copy(bf16[1,4,1578,2,192]{4,3,2,1,0:T(2,128)(2,1)} %bitcast.46) | data formatting | bytes 9695232 | tf_op jit(solution)/shard_map/all_to_all | solution.py:298
  819.1 5.3 all-gather.2.cloned.1.call-done
  824.4 9.0 fusion.13
  833.5 2.2 copy-done.5
  836.3 6.4 all-reduce.2
  842.8 37.9 %all-reduce.1 = (f32[2,2,192]{2,1,0:T(2,128)}, f32[2,768]{1,0:T(2,128)}, f32[2,2,192]{2,1,0:T(2,128)}, f32[5,192]{1,0:T(8,128)}, f32[5,192]{1,0:T(8,128)}) all-reduce(f32[2,2,192]{2,1,0:T(2,128)S(1)} %pad_maximum_fusion.2, f32[2,768]{1,0:T(2,128)S(1)} %pad_maximum_fusion.1, ...), channel_id=1, replica_groups=mesh['dp'=8,'head'=4] {'dp'}, use_global_device_ids=true, to_apply=%region_47.48 | all-reduce | flops 4992 | bytes 39936 | tf_op jit(solution)/shard_map/psum | solution.py:329
  880.7 5.3 fusion.16
  885.9 12.3 %reduce-scatter.24.cloned.1.call-done = f32[96,768]{1,0:T(8,128)} async-done(((f32[768,768]{1,0:T(8,128)}), f32[96,768]{1,0:T(8,128)}) %reduce-scatter.24.cloned.1.call-update) | async-done | bytes 294928 | tf_op jit(solution)/shard_map/reduce_scatter | solution.py:340
  898.2 72.9 %reduce-scatter.26.cloned.1.call-done = f32[768,96]{0,1:T(8,128)} async-done(((f32[768,768]{0,1:T(8,128)}), f32[768,96]{0,1:T(8,128)}) %reduce-scatter.26.cloned.1.call-update) | async-done | bytes 294928 | tf_op jit(solution)/shard_map/reduce_scatter | solution.py:341
  971.2 73.0 %reduce-scatter.20.cloned.1.call-done = f32[96,768]{1,0:T(8,128)} async-done(((f32[768,768]{1,0:T(8,128)}), f32[96,768]{1,0:T(8,128)}) %reduce-scatter.20.cloned.1.call-update) | async-done | bytes 294928 | tf_op jit(solution)/shard_map/reduce_scatter | solution.py:336
  1044.1 72.9 %reduce-scatter.22.cloned.1.call-done = f32[768,96]{0,1:T(8,128)} async-done(((f32[768,768]{0,1:T(8,128)}), f32[768,96]{0,1:T(8,128)}) %reduce-scatter.22.cloned.1.call-update) | async-done | bytes 294928 | tf_op jit(solution)/shard_map/reduce_scatter | solution.py:337
  (349 shorter events, 67.9 us)
Async XLA Ops:
  7.2 186.9 %copy-start = (bf16[768,768]{1,0:T(8,128)(2,1)S(1)}, bf16[768,768]{1,0:T(8,128)(2,1)}, u32[]{:S(2)}) copy-start(bf16[768,768]{1,0:T(8,128)(2,1)} %param.27) | copy-start | bytes 3538948
  7.2 182.4 %all-reduce.12.cloned.1.call-start = ((), (), s32[]{:S(2)}) async-start(), calls=%async_computation.10 | async-start | bytes 393216 | tf_op jit(solution)/shard_map/psum | solution.py:57
  7.3 53.6 %collective-permute-start = (bf16[1,1578,768]{2,1,0:T(8,128)(2,1)}, bf16[1,1578,768]{2,1,0:T(8,128)(2,1)}, u32[]{:S(2)}, u32[]{:S(2)}) collective-permute-start(bf16[1,1578,768]{2,1,0:T(8,128)(2,1)} %param.19), channel_id=1, source_target_pairs={{0,1},{1,2},{2,3},{3,0},{4,5},{5,6},{6,7},{7,4},{8,9},{9,10},{10,1... | collective-permute-start | bytes 7271432 | tf_op jit(solution)/shard_map/ppermute | solution.py:23
  7.8 88.3 %collective-permute-start.1 = (bf16[1,1578,768]{2,1,0:T(8,128)(2,1)}, bf16[1,1578,768]{2,1,0:T(8,128)(2,1)}, u32[]{:S(2)}, u32[]{:S(2)}) collective-permute-start(bf16[1,1578,768]{2,1,0:T(8,128)(2,1)} %param.19), channel_id=1, source_target_pairs={{0,3},{1,0},{2,1},{3,2},{4,7},{5,4},{6,5},{7,6},{8,11},{9,8},{10,9... | collective-permute-start | bytes 7271432 | tf_op jit(solution)/shard_map/ppermute | solution.py:28
  60.8 47.9 %collective-permute-start.2 = (bf16[1,1578,768]{2,1,0:T(8,128)(2,1)}, bf16[1,1578,768]{2,1,0:T(8,128)(2,1)}, u32[]{:S(2)}, u32[]{:S(2)}) collective-permute-start(bf16[1,1578,768]{2,1,0:T(8,128)(2,1)} %collective-permute-done), channel_id=1, source_target_pairs={{0,1},{1,2},{2,3},{3,0},{4,5},{5,6},{6,7},{7,4},{8,9},{9,10},{10,1... | collective-permute-start | bytes 7271432 | tf_op jit(solution)/shard_map/ppermute | solution.py:23
  64.1 85.6 %copy-start.92 = (f32[3,64]{1,0:T(4,128)}, f32[3,64]{1,0:T(4,128)S(1)}, u32[]{:S(2)}) copy-start(f32[3,64]{1,0:T(4,128)S(1)} %add.377) | copy-start | bytes 2308
  64.8 17.1 %copy-start.101 = (s32[1,40]{1,0:T(1,128)S(1)}, s32[1,40]{1,0:T(1,128)}, u32[]{:S(2)}) copy-start(s32[1,40]{1,0:T(1,128)} %param.21) | copy-start | bytes 484
  69.1 12.8 %copy-start.72 = (f32[2,2,768]{2,1,0:T(2,128)S(1)}, f32[2,2,768]{2,1,0:T(2,128)}, u32[]{:S(2)}) copy-start(f32[2,2,768]{2,1,0:T(2,128)} %param.34) | copy-start | bytes 36868
  69.1 13.5 %copy-start.73 = (f32[5,768]{1,0:T(8,128)S(1)}, f32[5,768]{1,0:T(8,128)}, u32[]{:S(2)}) copy-start(f32[5,768]{1,0:T(8,128)} %param.36) | copy-start | bytes 46084
  69.1 14.1 %copy-start.74 = (f32[5,768]{1,0:T(8,128)S(1)}, f32[5,768]{1,0:T(8,128)}, u32[]{:S(2)}) copy-start(f32[5,768]{1,0:T(8,128)} %param.35) | copy-start | bytes 46084
  69.1 14.2 %copy-start.3 = (bf16[1,128,768]{2,1,0:T(8,128)(2,1)S(1)}, bf16[1,128,768]{2,1,0:T(8,128)(2,1)}, u32[]{:S(2)}) copy-start(bf16[1,128,768]{2,1,0:T(8,128)(2,1)} %param.22) | copy-start | bytes 589828
  69.2 14.5 %copy-start.29 = (bf16[192,768]{1,0:T(8,128)(2,1)S(1)}, bf16[192,768]{1,0:T(8,128)(2,1)}, u32[]{:S(2)}) copy-start(bf16[192,768]{1,0:T(8,128)(2,1)} %param.23) | copy-start | bytes 884740
  83.2 25.5 %copy-start.60 = (f32[768]{0:T(1024)}, f32[768]{0:T(1024)S(1)}, u32[]{:S(2)}) copy-start(f32[768]{0:T(1024)S(1)} %get-tuple-element.152) | copy-start | bytes 9220
  83.2 49.9 %copy-start.88 = (f32[768]{0:T(1024)}, f32[768]{0:T(1024)S(1)}, u32[]{:S(2)}) copy-start(f32[768]{0:T(1024)S(1)} %get-tuple-element.153) | copy-start | bytes 9220
  83.2 108.7 %copy-start.47 = (f32[768]{0:T(1024)}, f32[768]{0:T(1024)S(1)}, u32[]{:S(2)}) copy-start(f32[768]{0:T(1024)S(1)} %get-tuple-element.151) | copy-start | bytes 9220
  83.3 25.4 %copy-start.40 = (f32[768]{0:T(1024)}, f32[768]{0:T(1024)S(1)}, u32[]{:S(2)}) copy-start(f32[768]{0:T(1024)S(1)} %get-tuple-element.147) | copy-start | bytes 9220
  83.3 49.8 %copy-start.44 = (f32[768]{0:T(1024)}, f32[768]{0:T(1024)S(1)}, u32[]{:S(2)}) copy-start(f32[768]{0:T(1024)S(1)} %get-tuple-element.148) | copy-start | bytes 9220
  83.4 25.3 %copy-start.70 = (f32[128]{0:T(128)}, f32[128]{0:T(128)S(1)}, u32[]{:S(2)}) copy-start(f32[128]{0:T(128)S(1)} %broadcast_multiply_fusion.6) | copy-start | bytes 1540
  83.7 25.1 %copy-start.95 = (f32[128]{0:T(128)}, f32[128]{0:T(128)S(1)}, u32[]{:S(2)}) copy-start(f32[128]{0:T(128)S(1)} %fusion.75) | copy-start | bytes 1540
  83.7 25.1 %copy-start.86 = (f32[128]{0:T(128)}, f32[128]{0:T(128)S(1)}, u32[]{:S(2)}) copy-start(f32[128]{0:T(128)S(1)} %fusion.120) | copy-start | bytes 1540
  84.0 54.7 %copy-start.31 = (bf16[128,192]{0,1:T(8,128)(2,1)}, bf16[128,192]{0,1:T(8,128)(2,1)S(1)}, u32[]{:S(2)}) copy-start(bf16[128,192]{0,1:T(8,128)(2,1)S(1)} %fusion.33) | copy-start | bytes 147460
  138.5 11.2 %copy-start.7 = (f32[1,6312,1,192]{1,3,2,0:T(8,128)}, f32[1,6312,1,192]{1,3,2,0:T(8,128)S(1)}, u32[]{:S(2)}) copy-start(f32[1,6312,1,192]{1,3,2,0:T(8,128)S(1)} %slice.107) | copy-start | bytes 14542852
  149.7 42.2 %copy-start.9 = (bf16[768,768]{1,0:T(8,128)(2,1)S(1)}, bf16[768,768]{1,0:T(8,128)(2,1)}, u32[]{:S(2)}) copy-start(bf16[768,768]{1,0:T(8,128)(2,1)} %param.26) | copy-start | bytes 3538948
  154.8 72.5 %copy-start.33 = (bf16[3,64,128]{2,1,0:T(8,128)(2,1)}, bf16[3,64,128]{2,1,0:T(8,128)(2,1)S(1)}, u32[]{:S(2)}) copy-start(bf16[3,64,128]{2,1,0:T(8,128)(2,1)S(1)} %fusion.34) | copy-start | bytes 147460
  154.8 72.5 %copy-start.62 = (f32[768]{0:T(1024)S(1)}, f32[768]{0:T(1024)}, u32[]{:S(2)}) copy-start(f32[768]{0:T(1024)} %get-tuple-element.156) | copy-start | bytes 9220
  154.8 73.9 %copy-start.50 = (f32[768]{0:T(1024)S(1)}, f32[768]{0:T(1024)}, u32[]{:S(2)}) copy-start(f32[768]{0:T(1024)} %get-tuple-element.154) | copy-start | bytes 9220
  155.8 71.5 %all-reduce.14.cloned.1.call-start = ((), (), s32[]{:S(2)}) async-start(), calls=%async_computation.11 | async-start | bytes 393216 | tf_op jit(solution)/shard_map/psum | solution.py:57
  189.6 37.7 %copy-start.6 = (bf16[1,128,768]{2,1,0:T(8,128)(2,1)S(1)}, bf16[1,128,768]{2,1,0:T(8,128)(2,1)}, u32[]{:S(2)}) copy-start(bf16[1,128,768]{2,1,0:T(8,128)(2,1)} %all-reduce.12.cloned.1.call-done) | copy-start | bytes 589828
  189.6 45.6 %copy-start.16 = (bf16[192,768]{1,0:T(8,128)(2,1)S(1)}, bf16[192,768]{1,0:T(8,128)(2,1)}, u32[]{:S(2)}) copy-start(bf16[192,768]{1,0:T(8,128)(2,1)} %param.29) | copy-start | bytes 884740
  190.8 36.5 %copy-start.52 = (f32[128]{0:T(128)}, f32[128]{0:T(128)S(1)}, u32[]{:S(2)}) copy-start(f32[128]{0:T(128)S(1)} %broadcast_multiply_fusion.5) | copy-start | bytes 1540
  191.9 35.4 %copy-start.97 = (f32[128]{0:T(128)}, f32[128]{0:T(128)S(1)}, u32[]{:S(2)}) copy-start(f32[128]{0:T(128)S(1)} %multiply_reduce_fusion.3) | copy-start | bytes 1540
  191.9 35.4 %copy-start.76 = (f32[128]{0:T(128)}, f32[128]{0:T(128)S(1)}, u32[]{:S(2)}) copy-start(f32[128]{0:T(128)S(1)} %fusion.121) | copy-start | bytes 1540
  194.0 77.1 %copy-start.8 = (bf16[768,768]{1,0:T(8,128)(2,1)S(1)}, bf16[768,768]{1,0:T(8,128)(2,1)}, u32[]{:S(2)}) copy-start(bf16[768,768]{1,0:T(8,128)(2,1)} %param.30) | copy-start | bytes 3538948
  195.1 74.1 %all-reduce.16.cloned.1.call-start = ((), (), s32[]{:S(2)}) async-start(), calls=%async_computation.12 | async-start | bytes 393216 | tf_op jit(solution)/shard_map/psum | solution.py:57
  231.0 38.2 %copy-start.27 = (bf16[1,128,1,192]{1,3,2,0:T(8,128)(2,1)}, bf16[1,128,1,192]{1,3,2,0:T(8,128)(2,1)S(1)}, u32[]{:S(2)}) copy-start(bf16[1,128,1,192]{1,3,2,0:T(8,128)(2,1)S(1)} %slice.134) | copy-start | bytes 147460
  231.8 37.4 %copy-start.28 = (bf16[128,3,64]{0,2,1:T(8,128)(2,1)}, bf16[128,3,64]{0,2,1:T(8,128)(2,1)S(1)}, u32[]{:S(2)}) copy-start(bf16[128,3,64]{0,2,1:T(8,128)(2,1)S(1)} %multiply_convert_fusion.4) | copy-start | bytes 147460
  237.0 72.7 %all-reduce.18.cloned.1.call-start = ((), (), s32[]{:S(2)}) async-start(), calls=%async_computation.13 | async-start | bytes 393216 | tf_op jit(solution)/shard_map/psum | solution.py:61
  277.4 82.7 %copy-start.99 = (f32[128]{0:T(128)S(1)}, f32[128]{0:T(128)}, u32[]{:S(2)}) copy-start(f32[128]{0:T(128)} %copy-done.98) | copy-start | bytes 1540
  277.4 82.7 %copy-start.55 = (f32[128]{0:T(128)S(1)}, f32[128]{0:T(128)}, u32[]{:S(2)}) copy-start(f32[128]{0:T(128)} %copy-done.54) | copy-start | bytes 1540
  277.4 82.7 %copy-start.79 = (f32[128]{0:T(128)S(1)}, f32[128]{0:T(128)}, u32[]{:S(2)}) copy-start(f32[128]{0:T(128)} %copy-done.78) | copy-start | bytes 1540
  277.5 80.8 %all-reduce.20.cloned.1.call-start = ((), (), s32[]{:S(2)}) async-start(), calls=%async_computation.14 | async-start | bytes 393216 | tf_op jit(solution)/shard_map/psum | solution.py:61
  311.4 52.3 %copy-start.12 = (f32[128,768]{1,0:T(8,128)S(1)}, f32[128,768]{1,0:T(8,128)}, u32[]{:S(2)}) copy-start(f32[128,768]{1,0:T(8,128)} %copy-done.11) | copy-start | bytes 1179652
  318.9 43.1 %copy-start.36 = (bf16[3,64,128]{2,1,0:T(8,128)(2,1)}, bf16[3,64,128]{2,1,0:T(8,128)(2,1)S(1)}, u32[]{:S(2)}) copy-start(bf16[3,64,128]{2,1,0:T(8,128)(2,1)S(1)} %get-tuple-element.197) | copy-start | bytes 147460
  322.2 39.8 %copy-start.23 = (bf16[3,64,128]{2,1,0:T(8,128)(2,1)}, bf16[3,64,128]{2,1,0:T(8,128)(2,1)S(1)}, u32[]{:S(2)}) copy-start(bf16[3,64,128]{2,1,0:T(8,128)(2,1)S(1)} %convolution_convert_fusion.11) | copy-start | bytes 147460
  323.9 38.1 %copy-start.25 = (bf16[3,64,128]{2,1,0:T(8,128)(2,1)}, bf16[3,64,128]{2,1,0:T(8,128)(2,1)S(1)}, u32[]{:S(2)}) copy-start(bf16[3,64,128]{2,1,0:T(8,128)(2,1)S(1)} %get-tuple-element.199) | copy-start | bytes 147460
  326.1 72.9 %all-reduce.22.cloned.1.call-start = ((), (), s32[]{:S(2)}) async-start(), calls=%async_computation.15 | async-start | bytes 393216 | tf_op jit(solution)/shard_map/psum | solution.py:61
  364.9 39.5 %copy-start.84 = (f32[3,128]{1,0:T(4,128)S(1)}, f32[3,128]{1,0:T(4,128)}, u32[]{:S(2)}) copy-start(f32[3,128]{1,0:T(4,128)} %copy-done.83) | copy-start | bytes 4612
  364.9 39.5 %copy-start.93 = (f32[3,64]{1,0:T(4,128)S(1)}, f32[3,64]{1,0:T(4,128)}, u32[]{:S(2)}) copy-start(f32[3,64]{1,0:T(4,128)} %copy-done.92) | copy-start | bytes 2308
  366.8 148.9 %all-reduce.24.cloned.1.call-start = ((), (), s32[]{:S(2)}) async-start(), calls=%async_computation.26 | async-start | bytes 786432 | tf_op jit(solution)/shard_map/psum | solution.py:57
  426.1 7.9 copy-start.34
  426.2 9.1 copy-start.32
  431.4 99.7 %reduce-scatter.36.cloned.1.call-start = ((), (), s32[]{:S(2)}) async-start(), calls=%async_computation.25 | async-start | bytes 884736
  432.7 164.0 %reduce-scatter.28.cloned.1.call-start = ((), (), s32[]{:S(2)}) async-start(), calls=%async_computation.21 | async-start | bytes 884736
  440.8 221.3 %reduce-scatter.32.cloned.1.call-start = ((), (), s32[]{:S(2)}) async-start(), calls=%async_computation.23 | async-start | bytes 884736
  447.9 281.5 %reduce-scatter.30.cloned.1.call-start = ((), (), s32[]{:S(2)}) async-start(), calls=%async_computation.22 | async-start | bytes 1327104
  467.8 332.0 %reduce-scatter.34.cloned.1.call-start = ((), (), s32[]{:S(2)}) async-start(), calls=%async_computation.24 | async-start | bytes 2211840
  478.6 345.8 %all-gather.2.cloned.1.call-start = ((), (), s32[]{:S(2)}) async-start(), calls=%async_computation.16 | async-start | bytes 2949120 | tf_op jit(solution)/shard_map/all_gather | solution.py:168
  479.4 418.9 %reduce-scatter.24.cloned.1.call-start = ((), (), s32[]{:S(2)}) async-start(), calls=%async_computation.19 | async-start | bytes 2654208 | tf_op jit(solution)/shard_map/reduce_scatter | solution.py:340
  481.4 489.7 %reduce-scatter.26.cloned.1.call-start = ((), (), s32[]{:S(2)}) async-start(), calls=%async_computation.20 | async-start | bytes 2654208 | tf_op jit(solution)/shard_map/reduce_scatter | solution.py:341
  483.5 560.6 %reduce-scatter.20.cloned.1.call-start = ((), (), s32[]{:S(2)}) async-start(), calls=%async_computation.17 | async-start | bytes 2654208 | tf_op jit(solution)/shard_map/reduce_scatter | solution.py:336
  507.2 294.6 %all-to-all-start = ((bf16[1,6312,2,192]{3,2,0,1:T(2,128)(2,1)}), bf16[1,6312,2,192]{3,2,0,1:T(2,128)(2,1)}, u32[]{:S(2)}, u32[]{:S(2)}) async-start(bf16[1,6312,2,192]{3,2,0,1:T(2,128)(2,1)} %copy.51), calls=%async_computation | async-start | bytes 12926976 | tf_op jit(solution)/shard_map/all_to_all | solution.py:298
  512.6 604.4 %reduce-scatter.22.cloned.1.call-start = ((), (), s32[]{:S(2)}) async-start(), calls=%async_computation.18 | async-start | bytes 2654208 | tf_op jit(solution)/shard_map/reduce_scatter | solution.py:337
  833.5 47.2 %copy-start.46 = (f32[768]{0:T(1024)S(1)}, f32[768]{0:T(1024)}, u32[]{:S(2)}) copy-start(f32[768]{0:T(1024)} %copy-done.44) | copy-start | bytes 9220
  880.7 236.4 %copy-start.1 = (bf16[768,768]{1,0:T(8,128)(2,1)S(1)}, bf16[768,768]{1,0:T(8,128)(2,1)}, u32[]{:S(2)}) copy-start(bf16[768,768]{1,0:T(8,128)(2,1)} %param.27) | copy-start | bytes 3538948
  (59 other events, 247.2 us)
Sparse Core Ops, SparseCore 0:
  155.9 33.7 all-reduce.11
  195.2 32.0 all-reduce.13
  237.1 32.0 all-reduce.15
  277.6 32.0 all-reduce.17
  326.2 32.0 all-reduce.19
  367.0 32.0 all-reduce.21
  431.5 32.8 all-reduce.23
  467.7 63.2 reduce-scatter.35
  534.4 62.2 reduce-scatter.27
  599.8 62.2 reduce-scatter.31
  665.5 63.8 reduce-scatter.29
  733.3 66.4 reduce-scatter.33
  801.4 23.0 all-gather.1
  828.3 69.8 reduce-scatter.23
  902.2 68.9 reduce-scatter.25
  975.1 68.9 reduce-scatter.19
  1048.0 68.9 reduce-scatter.21
